TPU v7x, 32 devices: a whole 2x2x4 slice. The times are simulated.
32 devices in a mesh: groups: 2 (over y), wide: 4 (over z), narrow: 4 (over x, core).
Axes of the slice: x: 2, y: 2, z: 4, core: 2. Of those that a mesh axis runs over, the one named last changes fastest.
Arguments:
- cont_queries: bfloat16 [32, 128, 64, 128], P(('groups', 'wide'), None, 'narrow'), parts along dimension 0, may hold values from -5 to 5
- cont_keys: bfloat16 [32, 128, 8, 128], P(('groups', 'wide'), None, 'narrow'), parts along dimension 0, may hold values from -5 to 5
- cont_values: bfloat16 [32, 128, 8, 128], P(('groups', 'wide'), None, 'narrow'), parts along dimension 0, may hold values from -5 to 5
- prefix_kv: bfloat16 [8, 2, 128, 8, 128], P(('groups', 'wide'), None, None, 'narrow'), parts along dimension 0, may hold values from -5 to 5
- probe: bfloat16 [64, 128], P('narrow'), may hold values from -0.5 to 0.5
- question_row: int32 [8], P('groups'), parts along dimension 0, may hold values from 0 to 3, each once
- cont_slot: int32 [32], P(('groups', 'wide')), parts along dimension 0, may hold values from 0 to 15, each once
- cont_length: int32 [32], P(('groups', 'wide')), parts along dimension 0, may hold values from 1 to 128
- gold: int32 [8], P('groups'), parts along dimension 0, may hold values from 0 to 3
Outputs:
- token_score: float32 [32, 128], P(('groups', 'wide')), parts along dimension 0
- owned_logprob: float32 [8, 4], P(('groups', 'wide')), parts along dimension 0
- owned_loss: float32 [8], P(('groups', 'wide')), parts along dimension 0
There are 2 independent parts, one for each index of `groups`. A program takes and returns all parts, laid end to end along the dimension named above; an argument that names none is the same for every part. Nothing has to cross between parts.
All inputs are finite; a program needn't handle non-finite values.
Results may differ from a plain program's by a relative error of at most 0.0065.
Values may be sent and summed in bfloat16 or wider, within the bound.
No kernel may reach another device: no remote copies, remote signals or barrier semaphores. Data moves between devices by JAX's collectives and lax.ppermute only.
A program may use at most 64 MiB of HBM per device.

v0:
```python
import jax
import jax.numpy as jnp
from jax import lax
from jax.sharding import PartitionSpec as P

ANSWERS = 4


def attend_part(queries, keys, values, allowed, scale_factor):
    scores = (
        jnp.einsum("ctkgd,cjkd->ckgtj", queries, keys, preferred_element_type=jnp.float32)
        * scale_factor
    )
    scores = jnp.where(allowed[None, None, None, :, :], scores, -jnp.inf)
    row_max = jnp.max(scores, axis=-1)
    expo = jnp.exp(scores - row_max[..., None])
    total = jnp.sum(expo, axis=-1)
    weights = expo.astype(jnp.bfloat16)
    summed = jnp.einsum("ckgtj,cjkd->ctkgd", weights, values, preferred_element_type=jnp.float32)
    return (row_max, total, summed)


def to_rows(stat):
    return jnp.transpose(stat, (0, 3, 1, 2))[..., None]


def per_device(
    cont_queries,
    cont_keys,
    cont_values,
    prefix_kv,
    probe,
    question_row,
    cont_slot,
    cont_length,
    gold,
):
    cont_count, clen, heads_here, head_dim = cont_queries.shape
    kv_here = cont_keys.shape[2]
    group_size = heads_here // kv_here
    quest_here = prefix_kv.shape[0]
    pref_len = prefix_kv.shape[2]
    questions = question_row.shape[0]
    scale_factor = 1.0 / head_dim**0.5
    wanted = question_row[cont_slot // ANSWERS]
    piece = lax.all_gather(prefix_kv, "wide", axis=0, tiled=True)
    count = piece.shape[0]
    hits = (wanted[:, None] == jnp.arange(count, dtype=jnp.int32)[None, :]).astype(jnp.bfloat16)
    chosen = jnp.einsum("cn,nkpvd->ckpvd", hits, piece, preferred_element_type=jnp.float32)
    mine = chosen.astype(jnp.bfloat16)
    queries = cont_queries.reshape(cont_count, clen, kv_here, group_size, head_dim)
    causal = jnp.arange(clen)[:, None] >= jnp.arange(clen)[None, :]
    keys_all = jnp.concatenate([mine[:, 0], cont_keys], axis=1)
    values_all = jnp.concatenate([mine[:, 1], cont_values], axis=1)
    allowed = jnp.concatenate([jnp.ones((clen, pref_len), dtype=bool), causal], axis=1)
    row_max, total, summed = attend_part(queries, keys_all, values_all, allowed, scale_factor)
    output = summed / to_rows(total)
    attended = output.astype(jnp.bfloat16).reshape(cont_count, clen, heads_here, head_dim)
    partial_value = jnp.einsum("cthd,hd->ct", attended, probe, preferred_element_type=jnp.float32)
    token_score = lax.psum(partial_value, "narrow")
    valid = jnp.arange(clen)[None, :] < cont_length[:, None]
    choice_score = jnp.sum(jnp.where(valid, token_score, 0.0), axis=1)
    target = wanted * ANSWERS + cont_slot % ANSWERS
    spots = target[:, None] == jnp.arange(questions * ANSWERS, dtype=jnp.int32)[None, :]
    term = jnp.sum(jnp.where(spots, choice_score[:, None], 0.0), axis=0).reshape(questions, ANSWERS)
    first_row = lax.axis_index("wide") * quest_here
    totals = lax.psum(term, "wide")
    owned = lax.dynamic_slice_in_dim(totals, first_row, quest_here, 0)
    logprob = owned - jax.nn.logsumexp(owned, axis=1, keepdims=True)
    owned_rows = first_row + jnp.arange(quest_here, dtype=jnp.int32)
    matches = question_row[None, :] == owned_rows[:, None]
    gold_owned = jnp.sum(jnp.where(matches, gold[None, :], 0), axis=1)
    answer_ids = jnp.arange(ANSWERS, dtype=jnp.int32)[None, :]
    owned_loss = -jnp.sum(jnp.where(answer_ids == gold_owned[:, None], logprob, 0.0), axis=1)
    return (token_score, logprob, owned_loss)


def solution(mesh):
    return jax.shard_map(
        per_device,
        mesh=mesh,
        in_specs=(
            P(("groups", "wide"), None, "narrow", None),
            P(("groups", "wide"), None, "narrow", None),
            P(("groups", "wide"), None, "narrow", None),
            P(("groups", "wide"), None, None, "narrow", None),
            P("narrow", None),
            P("groups"),
            P(("groups", "wide")),
            P(("groups", "wide")),
            P("groups"),
        ),
        out_specs=(P(("groups", "wide"), None), P(("groups", "wide"), None), P(("groups", "wide"))),
        check_vma=False,
    )
```

profile of v0, /device:TPU:0, one launch (start us, length us, event | category | flops | bytes accessed | tf_op | source)
XLA Modules:
  0.0 57.5 jit_solution(3568872146050696365)
XLA Ops:
  0.6 0.0 copy-start
  0.6 0.8 %compare_select_fusion = s32[4]{0:T(128)S(1)} fusion(s32[4]{0:T(128)} %param.15), kind=kLoop, calls=%fused_computation.27 | loop fusion | flops 72 | bytes 32 | tf_op jit(solution)/shard_map/select_n | solution.py:45
  1.5 1.3 %gather_fusion = s32[4]{0:T(128)S(1)} fusion(s32[4]{0:T(128)} %param.14, s32[1024]{0:T(1024)S(1)} %pad_clamp_fusion), kind=kCustom, calls=%fused_computation | custom fusion | bytes 48 | tf_op jit(solution)/shard_map/gather | solution.py:45
  2.8 0.9 %copy.34 = bf16[1,2,128,2,128]{4,2,3,1,0:T(8,128)(2,1)S(1)} copy(bf16[1,2,128,2,128]{4,3,2,1,0:T(2,128)(2,1)} %param.12) | data formatting | bytes 262144 | tf_op args[3]
  3.7 17.4 %all_gather.3 = bf16[4,2,128,2,128]{4,2,3,1,0:T(8,128)(2,1)S(1)} all-gather(bf16[1,2,128,2,128]{4,2,3,1,0:T(8,128)(2,1)S(1)} %copy.34), channel_id=1, replica_groups=mesh['groups'=2,'wide'=4,'narrow'=4] {'wide'}, dimensions={0}, use_global_device_ids=true | all-gather | bytes 655360 | tf_op jit(solution)/shard_map/all_gather | solution.py:46
  21.1 0.5 convolution_convert_fusion
  21.6 0.2 slice_bitcast_fusion.1
  21.8 1.3 %copy.36 = bf16[4,128,2,128]{3,0,2,1:T(4,128)(2,1)S(1)} copy(bf16[4,128,2,128]{3,2,1,0:T(2,128)(2,1)} %param.11) | data formatting | bytes 524288 | tf_op args[2]
  23.1 1.3 %copy.37 = bf16[4,128,2,128]{3,0,2,1:T(4,128)(2,1)S(1)} copy(bf16[4,128,2,128]{3,2,1,0:T(2,128)(2,1)} %param.10) | data formatting | bytes 524288 | tf_op args[1]
  24.4 0.7 %maximum_bitcast_fusion = (bf16[4,256,2,128,1]{3,0,2,1,4:T(4,128)(2,1)S(1)}, bf16[4,256,2,128,1]{3,0,2,1,4:T(4,128)(2,1)S(1)}) fusion(bf16[4,128,2,128]{3,0,2,1:T(4,128)(2,1)S(1)} %copy.36, bf16[4,128,2,128]{3,0,2,1:T(4,128)(2,1)S(1)} %get-tuple-element.5, bf16[4,128,2,128]{3,0,2,1:T(4,128)(2,1)S(1)} %copy.37, bf16[4,128,2,128]{3,0,2,1:T(4,128)(2,1)S(1)} %get-tuple-element.6), kind=kLoop, calls=%fused_computation.16 | loop fusion | flops 524288 | bytes 2097152 | tf_op jit(solution)/shard_map/concatenate | solution.py:54
  25.1 0.0 copy-done
  25.1 1.5 %fusion.2 = (f32[4,2,8,128]{3,2,1,0:T(8,128)S(1)}, f32[4,2,256,128,8]{3,2,4,1,0:T(8,128)S(1)}) fusion(pred[128,256]{0,1:T(8,128)(4,1)S(1)} %concatenate.10, bf16[4,128,2,8,128]{4,3,2,1,0:T(8,128)(2,1)S(1)} %bitcast.41, bf16[4,256,2,128,1]{3,0,2,1,4:T(4,128)(2,1)S(1)} %get-tuple-element.10), kind=kOutput, calls=%fused_computation.5 | convolution fusion | flops 543154176 | bytes 11075584 | tf_op jit(solution)/shard_map/ctkgd,cjkd->ckgtj/dot_general | solution.py:11
  26.7 2.2 %fusion = f32[4,2,8,128]{3,2,1,0:T(8,128)S(1)} fusion(f32[4,2,256,128,8]{3,2,4,1,0:T(8,128)S(1)} %get-tuple-element.8, f32[4,2,8,128]{3,2,1,0:T(8,128)S(1)} %get-tuple-element.7, pred[128,256]{0,1:T(8,128)(4,1)S(1)} %concatenate.10), kind=kLoop, calls=%fused_computation.3 | loop fusion | flops 8380416 | bytes 8486912 | tf_op jit(solution)/shard_map/reduce_sum | solution.py:17
  28.9 0.0 copy-start.2
  28.9 0.0 copy-start.4
  28.9 0.0 copy-start.6
  29.0 0.0 copy-start.1
  29.0 0.0 copy-start.5
  29.0 2.4 %fusion.5 = bf16[4,128,2,8,128]{1,4,3,2,0:T(8,128)(2,1)S(1)} fusion(f32[4,128,2,8]{1,3,2,0:T(8,128)S(1)} %bitcast.43, f32[4,2,256,128,8]{3,2,4,1,0:T(8,128)S(1)} %get-tuple-element.8, f32[4,2,8,128]{3,2,1,0:T(8,128)S(1)} %get-tuple-element.7, pred[128,256]{0,1:T(8,128)(4,1)S(1)} %concatenate.10, bf16[4,256,2,128,1]{3,0,2,1,4:T(4,128)(2,1)S(1)} %get-tuple-element.9), kind=kOutput, calls=%fused_computation.8 | convolution fusion | flops 547356672 | bytes 11108352 | tf_op jit(solution)/shard_map/ckgtj,cjkd->ctkgd/dot_general | solution.py:19
  31.3 0.0 copy-done.2
  31.3 0.4 fusion.17
  31.7 5.6 %psum.14 = f32[4,128]{1,0:T(4,128)S(1)} all-reduce(f32[4,128]{1,0:T(4,128)S(1)} %bitcast.45), channel_id=1, replica_groups=mesh['groups'=2,'wide'=4,'narrow'=4] {'narrow'}, use_global_device_ids=true, to_apply=%region_2.3 | all-reduce | flops 512 | bytes 4096 | tf_op jit(solution)/shard_map/psum | solution.py:60
  37.4 0.0 copy-done.4
  37.4 0.0 copy-start.3
  37.4 0.2 select_reduce_fusion.1
  37.6 0.0 copy-done.6
  37.6 0.1 select_reduce_fusion
  37.7 0.1 reshape.54
  37.7 12.5 %psum.15 = f32[4,4]{1,0:T(4,128)S(1)} all-reduce(f32[4,4]{1,0:T(4,128)S(1)} %reshape.54), channel_id=1, replica_groups=mesh['groups'=2,'wide'=4,'narrow'=4] {'wide'}, use_global_device_ids=true, to_apply=%region_5.6 | all-reduce | flops 16 | bytes 128 | tf_op jit(solution)/shard_map/psum | solution.py:67
  50.2 0.6 %fusion.27 = f32[]{:T(128)} fusion(f32[4,4]{1,0:T(4,128)S(1)} %psum.15, s32[]{:T(128)S(6)} %select_n.48), kind=kLoop, calls=%fused_computation.50 | loop fusion | flops 3 | bytes 24 | tf_op jit(solution)/shard_map/reduce_max | solution.py:69
  52.1 0.6 %exponential_reduce_fusion = f32[]{:T(128)} fusion(f32[]{:T(128)} %bitcast.15, f32[4,4]{1,0:T(4,128)S(1)} %psum.15, s32[]{:T(128)S(6)} %select_n.48), kind=kLoop, calls=%fused_computation.45 | loop fusion | flops 7 | bytes 28 | tf_op jit(solution)/shard_map/reduce_sum | solution.py:69
  53.4 0.0 copy-done.1
  53.4 0.0 copy-done.5
  53.4 0.6 %fusion.23 = s32[]{:T(128)} fusion(s32[4]{0:T(128)S(1)} %copy-done.5, s32[4]{0:T(128)S(1)} %copy-done.1, s32[]{:T(128)S(6)} %axis_index.15), kind=kLoop, calls=%fused_computation.43 | loop fusion | flops 11 | bytes 40 | tf_op jit(solution)/shard_map/reduce_sum | solution.py:72
  54.1 1.8 %fusion.24 = (f32[]{:T(128)}, f32[1,4]{1,0:T(1,128)}) fusion(s32[]{:T(128)} %fusion.23, f32[]{:T(128)} %bitcast.17, f32[4,4]{1,0:T(4,128)S(1)} %psum.15, s32[]{:T(128)S(6)} %select_n.48), kind=kLoop, calls=%fused_computation.44 | loop fusion | flops 15 | bytes 48 | tf_op jit(solution)/shard_map/reduce_sum | solution.py:74
  56.4 0.0 copy-done.3
  (4 shorter events, 0.0 us)
Async XLA Ops:
  0.6 24.5 %copy-start = (bf16[4,128,16,128]{3,2,1,0:T(8,128)(2,1)S(1)}, bf16[4,128,16,128]{3,2,1,0:T(8,128)(2,1)}, u32[]{:S(2)}) copy-start(bf16[4,128,16,128]{3,2,1,0:T(8,128)(2,1)} %param.9) | copy-start | bytes 6291460
  28.9 2.4 %copy-start.2 = (bf16[16,128]{1,0:T(8,128)(2,1)S(1)}, bf16[16,128]{1,0:T(8,128)(2,1)}, u32[]{:S(2)}) copy-start(bf16[16,128]{1,0:T(8,128)(2,1)} %param.13) | copy-start | bytes 12292
  28.9 8.4 %copy-start.4 = (s32[4]{0:T(128)S(1)}, s32[4]{0:T(128)}, u32[]{:S(2)}) copy-start(s32[4]{0:T(128)} %param.16) | copy-start | bytes 52
  28.9 8.6 %copy-start.6 = (s32[4]{0:T(128)S(1)}, s32[4]{0:T(128)}, u32[]{:S(2)}) copy-start(s32[4]{0:T(128)} %param.15) | copy-start | bytes 52
  29.0 24.5 %copy-start.1 = (s32[4]{0:T(128)S(1)}, s32[4]{0:T(128)}, u32[]{:S(2)}) copy-start(s32[4]{0:T(128)} %param.14) | copy-start | bytes 52
  29.0 24.5 %copy-start.5 = (s32[4]{0:T(128)S(1)}, s32[4]{0:T(128)}, u32[]{:S(2)}) copy-start(s32[4]{0:T(128)} %param.17) | copy-start | bytes 52
  37.4 19.0 %copy-start.3 = (f32[4,128]{1,0:T(4,128)}, f32[4,128]{1,0:T(4,128)S(1)}, u32[]{:S(2)}) copy-start(f32[4,128]{1,0:T(4,128)S(1)} %psum.14) | copy-start | bytes 6148
where the time goes:
time: 57.8 us; the launch traced here: 57.5 us
  blocking collectives  35.5 us (61%)
  other arithmetic  7.63 us (13%)
  local copies, waits for them, and re-layouts  5.13 us (9%)
  matrix products  4.82 us (8%)
  between operations  4.47 us (8%)
    all_gather x1, blocking collectives, per_device(): piece = lax.all_gather(prefix_kv, 'wide', axis=0, tiled=True)  17.4 us
    psum x1, blocking collectives, per_device(): totals = lax.psum(term, 'wide')  12.5 us
    psum x1, blocking collectives, per_device(): token_score = lax.psum(partial_value, 'narrow')  5.64 us
    unnamed x17, local copies, waits for them, and re-layouts  3.56 us
    dot_general x1, matrix products, attend_part(): jnp.einsum('ckgtj,cjkd->ctkgd', weights, values, preferred_element_type=j...  2.35 us
    reduce_sum x1, other arithmetic, attend_part(): total = jnp.sum(expo, axis=-1)  2.23 us
    reduce_sum x1, other arithmetic, per_device(): jnp.sum(jnp.where(answer_ids == gold_owned[:, None], logprob, 0.0), axis=1)  1.75 us
    dot_general x1, matrix products, attend_part(): jnp.einsum('ctkgd,cjkd->ckgtj', queries, keys, preferred_element_type=jnp...  1.54 us

commit v1 on v0

--- a/solution.py
+++ b/solution.py
@@ -64,7 +64,9 @@
     spots = target[:, None] == jnp.arange(questions * ANSWERS, dtype=jnp.int32)[None, :]
     term = jnp.sum(jnp.where(spots, choice_score[:, None], 0.0), axis=0).reshape(questions, ANSWERS)
     first_row = lax.axis_index("wide") * quest_here
-    totals = lax.psum(term, "wide")
+    totals = term
+    for hop in (1, 2):
+        totals = totals + lax.ppermute(totals, "wide", [(dev, dev ^ hop) for dev in range(4)])
     owned = lax.dynamic_slice_in_dim(totals, first_row, quest_here, 0)
     logprob = owned - jax.nn.logsumexp(owned, axis=1, keepdims=True)
     owned_rows = first_row + jnp.arange(quest_here, dtype=jnp.int32)

time: 57.8 us -> 53.7 us (0.929)
  blocking collectives: 35.5 us -> 23 us
  starting transfers between devices: 0 us -> 4.69 us
  waiting for transfers between devices: 0 us -> 2.86 us
  other arithmetic: 7.63 us -> 8.37 us
    psum x1 -> x0, blocking collectives: 12.5 us -> none  [per_device(): totals = lax.psum(term, 'wide')]
    ppermute x0 -> x2, starting transfers between devices: none -> 4.69 us  [per_device(): lax.ppermute(totals, 'wide', [(dev, dev ^ hop) for dev in range(4)])]
    ppermute x0 -> x2, waiting for transfers between devices: none -> 2.86 us  [per_device(): lax.ppermute(totals, 'wide', [(dev, dev ^ hop) for dev in range(4)])]
    add x1, other arithmetic: 0.01 us -> 0.67 us  [per_device(): target = wanted * ANSWERS + cont_slot % ANSWERS]
    unnamed x17 -> x15, local copies, waits for them, and re-layouts: 3.56 us -> 3.55 us
  transfers between devices with their start and end apart: 0 -> 2, of which waited for: 0 -> 2; matrix products, arithmetic and copies ran while one was open for 0% -> 1% of each run, Pallas kernels for 0% -> 0%
where the time goes in v1:
time: 53.7 us; the launch traced here: 53.4 us
  blocking collectives  23 us (43%)
  other arithmetic  8.37 us (16%)
  local copies, waits for them, and re-layouts  5.12 us (10%)
  matrix products  4.82 us (9%)
  starting transfers between devices  4.69 us (9%)
  between operations  4.49 us (8%)
  waiting for transfers between devices  2.86 us (5%)
    all_gather x1, blocking collectives, per_device(): piece = lax.all_gather(prefix_kv, 'wide', axis=0, tiled=True)  17.4 us
    psum x1, blocking collectives, per_device(): token_score = lax.psum(partial_value, 'narrow')  5.64 us
    ppermute x2, starting transfers between devices, per_device(): lax.ppermute(totals, 'wide', [(dev, dev ^ hop) for dev in range(4)])  4.69 us
    unnamed x15, local copies, waits for them, and re-layouts  3.55 us
    ppermute x2, waiting for transfers between devices, per_device(): lax.ppermute(totals, 'wide', [(dev, dev ^ hop) for dev in range(4)])  2.86 us
    dot_general x1, matrix products, attend_part(): jnp.einsum('ckgtj,cjkd->ctkgd', weights, values, preferred_element_type=j...  2.35 us
    reduce_sum x1, other arithmetic, attend_part(): total = jnp.sum(expo, axis=-1)  2.23 us
    reduce_sum x1, other arithmetic, per_device(): jnp.sum(jnp.where(answer_ids == gold_owned[:, None], logprob, 0.0), axis=1)  1.76 us
  transfers between devices with their start and end apart: 2, of which 2 were waited for; matrix products, arithmetic and copies ran while one was open for 1% of the time, Pallas kernels for 0%

profile of v1, /device:TPU:0, one launch (start us, length us, event | category | flops | bytes accessed | tf_op | source)
XLA Modules:
  0.0 53.4 jit_solution(4943295451239697367)
XLA Ops:
  0.6 0.0 copy-start
  0.7 0.8 %compare_select_fusion = s32[4]{0:T(128)S(1)} fusion(s32[4]{0:T(128)} %param.15), kind=kLoop, calls=%fused_computation.27 | loop fusion | flops 72 | bytes 32 | tf_op jit(solution)/shard_map/select_n | solution.py:45
  1.5 0.9 %copy.34 = bf16[1,2,128,2,128]{4,2,3,1,0:T(8,128)(2,1)S(1)} copy(bf16[1,2,128,2,128]{4,3,2,1,0:T(2,128)(2,1)} %param.12) | data formatting | bytes 262144 | tf_op args[3]
  2.4 17.4 %all_gather.3 = bf16[4,2,128,2,128]{4,2,3,1,0:T(8,128)(2,1)S(1)} all-gather(bf16[1,2,128,2,128]{4,2,3,1,0:T(8,128)(2,1)S(1)} %copy.34), channel_id=1, replica_groups=mesh['groups'=2,'wide'=4,'narrow'=4] {'wide'}, dimensions={0}, use_global_device_ids=true | all-gather | bytes 655360 | tf_op jit(solution)/shard_map/all_gather | solution.py:46
  19.8 1.3 %gather_fusion = s32[4]{0:T(128)S(1)} fusion(s32[4]{0:T(128)} %param.14, s32[1024]{0:T(1024)S(1)} %pad_clamp_fusion), kind=kCustom, calls=%fused_computation | custom fusion | bytes 48 | tf_op jit(solution)/shard_map/gather | solution.py:45
  21.1 0.7 %fusion.22 = s32[4]{0:T(128)S(1)} fusion(s32[4]{0:T(128)S(1)} %gather_fusion, s32[4]{0:T(128)} %param.15), kind=kLoop, calls=%fused_computation.42 | loop fusion | flops 52 | bytes 48 | tf_op jit(solution)/shard_map/add | solution.py:63
  21.7 0.5 %convolution_convert_fusion = bf16[4,2,128,2,128]{4,0,3,2,1:T(4,128)(2,1)S(1)} fusion(bf16[4,2,128,2,128]{4,2,3,1,0:T(8,128)(2,1)S(1)} %all_gather.3, s32[4]{0:T(128)S(1)} %gather_fusion), kind=kOutput, calls=%fused_computation.15 | convolution fusion | flops 2359312 | bytes 1048592 | tf_op jit(solution)/shard_map/cn,nkpvd->ckpvd/dot_general | solution.py:49
  22.3 0.2 slice_bitcast_fusion.1
  22.5 1.3 %copy.36 = bf16[4,128,2,128]{3,0,2,1:T(4,128)(2,1)S(1)} copy(bf16[4,128,2,128]{3,2,1,0:T(2,128)(2,1)} %param.11) | data formatting | bytes 524288 | tf_op args[2]
  23.8 1.3 %copy.37 = bf16[4,128,2,128]{3,0,2,1:T(4,128)(2,1)S(1)} copy(bf16[4,128,2,128]{3,2,1,0:T(2,128)(2,1)} %param.10) | data formatting | bytes 524288 | tf_op args[1]
  25.1 0.7 %maximum_bitcast_fusion = (bf16[4,256,2,128,1]{3,0,2,1,4:T(4,128)(2,1)S(1)}, bf16[4,256,2,128,1]{3,0,2,1,4:T(4,128)(2,1)S(1)}) fusion(bf16[4,128,2,128]{3,0,2,1:T(4,128)(2,1)S(1)} %copy.36, bf16[4,128,2,128]{3,0,2,1:T(4,128)(2,1)S(1)} %get-tuple-element.5, bf16[4,128,2,128]{3,0,2,1:T(4,128)(2,1)S(1)} %copy.37, bf16[4,128,2,128]{3,0,2,1:T(4,128)(2,1)S(1)} %get-tuple-element.6), kind=kLoop, calls=%fused_computation.16 | loop fusion | flops 524288 | bytes 2097152 | tf_op jit(solution)/shard_map/concatenate | solution.py:54
  25.8 0.0 copy-done
  25.8 1.5 %fusion.2 = (f32[4,2,8,128]{3,2,1,0:T(8,128)S(1)}, f32[4,2,256,128,8]{3,2,4,1,0:T(8,128)S(1)}) fusion(pred[128,256]{0,1:T(8,128)(4,1)S(1)} %concatenate.10, bf16[4,128,2,8,128]{4,3,2,1,0:T(8,128)(2,1)S(1)} %bitcast.41, bf16[4,256,2,128,1]{3,0,2,1,4:T(4,128)(2,1)S(1)} %get-tuple-element.10), kind=kOutput, calls=%fused_computation.5 | convolution fusion | flops 543154176 | bytes 11075584 | tf_op jit(solution)/shard_map/ctkgd,cjkd->ckgtj/dot_general | solution.py:11
  27.3 2.2 %fusion = f32[4,2,8,128]{3,2,1,0:T(8,128)S(1)} fusion(f32[4,2,256,128,8]{3,2,4,1,0:T(8,128)S(1)} %get-tuple-element.8, f32[4,2,8,128]{3,2,1,0:T(8,128)S(1)} %get-tuple-element.7, pred[128,256]{0,1:T(8,128)(4,1)S(1)} %concatenate.10), kind=kLoop, calls=%fused_computation.3 | loop fusion | flops 8380416 | bytes 8486912 | tf_op jit(solution)/shard_map/reduce_sum | solution.py:17
  29.6 0.0 copy-start.2
  29.6 0.0 copy-start.4
  29.6 0.0 copy-start.1
  29.6 0.0 copy-start.5
  29.6 2.4 %fusion.5 = bf16[4,128,2,8,128]{1,4,3,2,0:T(8,128)(2,1)S(1)} fusion(f32[4,128,2,8]{1,3,2,0:T(8,128)S(1)} %bitcast.43, f32[4,2,256,128,8]{3,2,4,1,0:T(8,128)S(1)} %get-tuple-element.8, f32[4,2,8,128]{3,2,1,0:T(8,128)S(1)} %get-tuple-element.7, pred[128,256]{0,1:T(8,128)(4,1)S(1)} %concatenate.10, bf16[4,256,2,128,1]{3,0,2,1,4:T(4,128)(2,1)S(1)} %get-tuple-element.9), kind=kOutput, calls=%fused_computation.8 | convolution fusion | flops 547356672 | bytes 11108352 | tf_op jit(solution)/shard_map/ckgtj,cjkd->ctkgd/dot_general | solution.py:19
  32.0 0.0 copy-done.2
  32.0 0.4 fusion.17
  32.4 5.6 %psum.7 = f32[4,128]{1,0:T(4,128)S(1)} all-reduce(f32[4,128]{1,0:T(4,128)S(1)} %bitcast.45), channel_id=1, replica_groups=mesh['groups'=2,'wide'=4,'narrow'=4] {'narrow'}, use_global_device_ids=true, to_apply=%region_2.3 | all-reduce | flops 512 | bytes 4096 | tf_op jit(solution)/shard_map/psum | solution.py:60
  38.0 0.0 copy-done.4
  38.0 0.0 copy-start.3
  38.0 0.2 select_reduce_fusion.1
  38.2 0.1 select_reduce_fusion
  38.3 0.1 reshape.54
  38.4 2.1 %collective-permute-start = (f32[4,4]{1,0:T(4,128)S(1)}, f32[4,4]{1,0:T(4,128)S(1)}, u32[]{:S(2)}, u32[]{:S(2)}) collective-permute-start(f32[4,4]{1,0:T(4,128)S(1)} %reshape.54), channel_id=1, source_target_pairs={{0,4},{4,0},{8,12},{12,8},{1,5},{5,1},{9,13},{13,9},{2,6},{6,2},{1... | collective-permute-start | bytes 200 | tf_op jit(solution)/shard_map/ppermute | solution.py:69
  40.5 0.0 copy-done.1
  40.5 0.0 copy-done.5
  40.5 0.6 %fusion.23 = s32[]{:T(128)} fusion(s32[4]{0:T(128)S(1)} %copy-done.5, s32[4]{0:T(128)S(1)} %copy-done.1, s32[]{:T(128)S(6)} %axis_index.15), kind=kLoop, calls=%fused_computation.43 | loop fusion | flops 11 | bytes 40 | tf_op jit(solution)/shard_map/reduce_sum | solution.py:74
  41.2 0.9 %collective-permute-done = f32[4,4]{1,0:T(4,128)S(1)} collective-permute-done((f32[4,4]{1,0:T(4,128)S(1)}, f32[4,4]{1,0:T(4,128)S(1)}, u32[]{:S(2)}, u32[]{:S(2)}) %collective-permute-start) | collective-permute-done | bytes 96 | tf_op jit(solution)/shard_map/ppermute | solution.py:69
  42.1 2.5 %collective-permute-start.1 = (f32[4,4]{1,0:T(4,128)S(1)}, f32[4,4]{1,0:T(4,128)S(1)}, u32[]{:S(2)}, u32[]{:S(2)}) collective-permute-start(f32[4,4]{1,0:T(4,128)S(1)} %add.30), channel_id=1, source_target_pairs={{0,8},{4,12},{8,0},{12,4},{1,9},{5,13},{9,1},{13,5},{2,10},{6,14},... | collective-permute-start | bytes 200 | tf_op jit(solution)/shard_map/ppermute | solution.py:69
  44.6 1.9 %collective-permute-done.1 = f32[4,4]{1,0:T(4,128)S(1)} collective-permute-done((f32[4,4]{1,0:T(4,128)S(1)}, f32[4,4]{1,0:T(4,128)S(1)}, u32[]{:S(2)}, u32[]{:S(2)}) %collective-permute-start.1) | collective-permute-done | bytes 96 | tf_op jit(solution)/shard_map/ppermute | solution.py:69
  46.6 0.6 %fusion.27 = f32[]{:T(128)} fusion(f32[4,4]{1,0:T(4,128)S(1)} %add.31, s32[]{:T(128)S(6)} %select_n.48), kind=kLoop, calls=%fused_computation.50 | loop fusion | flops 3 | bytes 24 | tf_op jit(solution)/shard_map/reduce_max | solution.py:71
  48.5 0.7 %exponential_reduce_fusion = f32[]{:T(128)} fusion(f32[]{:T(128)} %bitcast.15, f32[4,4]{1,0:T(4,128)S(1)} %add.31, s32[]{:T(128)S(6)} %select_n.48), kind=kLoop, calls=%fused_computation.45 | loop fusion | flops 7 | bytes 28 | tf_op jit(solution)/shard_map/reduce_sum | solution.py:71
  49.9 1.8 %fusion.24 = (f32[]{:T(128)}, f32[1,4]{1,0:T(1,128)}) fusion(s32[]{:T(128)} %fusion.23, f32[]{:T(128)} %bitcast.17, f32[4,4]{1,0:T(4,128)S(1)} %add.31, s32[]{:T(128)S(6)} %select_n.48), kind=kLoop, calls=%fused_computation.44 | loop fusion | flops 15 | bytes 48 | tf_op jit(solution)/shard_map/reduce_sum | solution.py:76
  52.2 0.0 copy-done.3
  (5 shorter events, 0.0 us)
Async XLA Ops:
  0.6 25.2 %copy-start = (bf16[4,128,16,128]{3,2,1,0:T(8,128)(2,1)S(1)}, bf16[4,128,16,128]{3,2,1,0:T(8,128)(2,1)}, u32[]{:S(2)}) copy-start(bf16[4,128,16,128]{3,2,1,0:T(8,128)(2,1)} %param.9) | copy-start | bytes 6291460
  29.6 2.4 %copy-start.2 = (bf16[16,128]{1,0:T(8,128)(2,1)S(1)}, bf16[16,128]{1,0:T(8,128)(2,1)}, u32[]{:S(2)}) copy-start(bf16[16,128]{1,0:T(8,128)(2,1)} %param.13) | copy-start | bytes 12292
  29.6 8.4 %copy-start.4 = (s32[4]{0:T(128)S(1)}, s32[4]{0:T(128)}, u32[]{:S(2)}) copy-start(s32[4]{0:T(128)} %param.16) | copy-start | bytes 52
  29.6 10.9 %copy-start.1 = (s32[4]{0:T(128)S(1)}, s32[4]{0:T(128)}, u32[]{:S(2)}) copy-start(s32[4]{0:T(128)} %param.14) | copy-start | bytes 52
  29.6 10.9 %copy-start.5 = (s32[4]{0:T(128)S(1)}, s32[4]{0:T(128)}, u32[]{:S(2)}) copy-start(s32[4]{0:T(128)} %param.17) | copy-start | bytes 52
  38.0 14.2 %copy-start.3 = (f32[4,128]{1,0:T(4,128)}, f32[4,128]{1,0:T(4,128)S(1)}, u32[]{:S(2)}) copy-start(f32[4,128]{1,0:T(4,128)S(1)} %psum.7) | copy-start | bytes 6148
  38.4 3.7 %collective-permute-start = (f32[4,4]{1,0:T(4,128)S(1)}, f32[4,4]{1,0:T(4,128)S(1)}, u32[]{:S(2)}, u32[]{:S(2)}) collective-permute-start(f32[4,4]{1,0:T(4,128)S(1)} %reshape.54), channel_id=1, source_target_pairs={{0,4},{4,0},{8,12},{12,8},{1,5},{5,1},{9,13},{13,9},{2,6},{6,2},{1... | collective-permute-start | bytes 200 | tf_op jit(solution)/shard_map/ppermute | solution.py:69
  42.1 4.5 %collective-permute-start.1 = (f32[4,4]{1,0:T(4,128)S(1)}, f32[4,4]{1,0:T(4,128)S(1)}, u32[]{:S(2)}, u32[]{:S(2)}) collective-permute-start(f32[4,4]{1,0:T(4,128)S(1)} %add.30), channel_id=1, source_target_pairs={{0,8},{4,12},{8,0},{12,4},{1,9},{5,13},{9,1},{13,5},{2,10},{6,14},... | collective-permute-start | bytes 200 | tf_op jit(solution)/shard_map/ppermute | solution.py:69
